TPU v7x, 32 devices: a whole 2x2x4 slice. The times are simulated.
32 devices in a mesh: row: 4 (over z), col: 8 (over y, x, core).
Axes of the slice: x: 2, y: 2, z: 4, core: 2. Of those that a mesh axis runs over, the one named last changes fastest.
Arguments:
- working: float32 [16, 4, 256, 8, 8, 256], P(None, 'row', None, None, 'col'), may hold values from -6 to 6
- factor_panel: float32 [2, 16, 4, 256, 256], P(None, None, 'row'), may hold values from -0.12 to 2, as said below
Outputs:
- gram_part: float32 [16, 4, 256, 8, 8, 256], P(None, 'row', None, None, 'col')
- finished_columns: float32 [8, 4, 256, 8, 4, 512], P(None, None, None, 'col', 'row')
Inputs may be any that keep to these rules, and one draw needn't show every extreme that they name: factor_panel holds a lower-triangular factor: entries above the factor's diagonal are zero and its diagonal entries lie between 1 and 2.
All inputs are finite; a program needn't handle non-finite values.
Results may differ from a plain program's by a relative error of at most 0.0001.
Values sent between devices are 32-bit elements; how exact they have to be, the bound alone decides.
No kernel may reach another device: no remote copies, remote signals or barrier semaphores. Data moves between devices by JAX's collectives and lax.ppermute only.
A program may use at most 256 MiB of HBM per device.

v0:
```python
import jax
import jax.numpy as jnp
from jax import lax
from jax.sharding import PartitionSpec as P

BLK = 256
K = 30
STEPS = 2


def from_root(value, axis, source):
    kept = jnp.where(lax.axis_index(axis) == source, value, 0).astype(value.dtype)
    return lax.psum(kept, axis)


def per_device(working, factor_panel):
    row_count = lax.axis_size("row")
    col_count = lax.axis_size("col")
    row_index = lax.axis_index("row")
    blocks_rows = working.shape[0]
    width = working.shape[2]
    blocks_cols = working.shape[3]
    matrix_rows = working.reshape(blocks_rows, width, blocks_cols * width)
    global_block = jnp.arange(blocks_rows) * row_count + row_index
    solved_list = []
    for step_index in range(STEPS):
        target = K + step_index
        slab = matrix_rows[target // row_count]
        solve_target = K + step_index
        owner = solve_target % row_count
        diagonal = jnp.tril(factor_panel[step_index, solve_target // row_count, 0])
        diagonal = jnp.where(row_index == owner, diagonal, jnp.eye(width, dtype=jnp.float32))
        solve_solved = lax.linalg.triangular_solve(diagonal, slab, left_side=True, lower=True)
        solved = from_root(solve_solved, "row", owner)
        column_part = factor_panel[step_index, :, 0]
        eliminate_target = K + step_index
        updated = matrix_rows - jnp.einsum(
            "rab,bc->rac", column_part, solved, precision=lax.Precision.HIGHEST
        )
        below = (global_block > eliminate_target)[:, None, None]
        here = (global_block == eliminate_target)[:, None, None]
        matrix_rows = jnp.where(below, updated, jnp.where(here, solved[None], matrix_rows))
        solved_list.append(solved)
    stacked = jnp.concatenate(solved_list, 0)
    depth = stacked.shape[0]
    owners_count = col_count // row_count
    pieces = [
        from_root(stacked.reshape(depth, blocks_cols, width), "col", row_index + offset * row_count)
        for offset in range(owners_count)
    ]
    chosen = jnp.stack(pieces, 2)
    row_panels = chosen.reshape(depth, blocks_rows * width)
    gram = lax.dot_general(
        row_panels, stacked, (((0,), (0,)), ((), ())), precision=lax.Precision.HIGHEST
    )
    gram = (gram * (1.0 / (STEPS * BLK))).reshape(blocks_rows, 1, width, blocks_cols, 1, width)
    finished_count = (K + STEPS) // row_count
    finished = matrix_rows[:finished_count].reshape(finished_count, 1, width, 1, row_count, -1)
    moved = lax.all_to_all(finished, "row", split_axis=4, concat_axis=1, tiled=True)
    return (gram, moved)


def solution(mesh):
    placed = (P(None, "row", None, None, "col", None), P(None, None, "row", None, None))
    return jax.shard_map(
        per_device,
        mesh=mesh,
        in_specs=placed,
        out_specs=(
            P(None, "row", None, None, "col", None),
            P(None, None, None, "col", "row", None),
        ),
        check_vma=False,
    )
```

profile of v0, /device:TPU:0, one launch (start us, length us, event | category | flops | bytes accessed | tf_op | source)
XLA Modules:
  0.0 810.8 jit_solution(15085424552516502196)
XLA Ops:
  7.2 1.1 fusion.9
  8.3 0.1 broadcast.96
  8.4 4.0 while.4
  8.4 0.6 fusion.24
  9.0 1.4 bitcast_dynamic-update-slice_fusion.4
  10.4 0.6 fusion.24
  11.0 1.4 bitcast_dynamic-update-slice_fusion.4
  12.4 19.7 %custom-call.4 = f32[2,128,128]{1,2,0:T(8,128)S(1)} custom-call(f32[2,128,128]{2,1,0:T(8,128)S(1)} %get-tuple-element.17), custom_call_target="InvertDiagBlocksLowerTriangular" | custom-call | tf_op jit(solution)/shard_map/triangular_solve/custom-call.1 | solution.py:33
  32.1 7.2 slice_reduce_fusion
  39.2 0.9 copy.44
  40.1 1.1 fusion.6
  41.2 1.0 convolution_subtract_fusion.1
  42.2 1.1 fusion.13
  43.3 1.5 maximum_select_fusion
  44.8 0.0 all-reduce.7.cloned.1.call-start
  44.8 79.1 %copy.24 = f32[16,1,256,8,1,256]{2,5,3,0,4,1:T(8,128)} copy(f32[16,1,256,8,1,256]{5,4,3,2,1,0:T(1,128)} %param.4) | data formatting | bytes 67108864 | tf_op args[0]
  123.9 3.8 while.5
  123.9 0.6 fusion.25
  124.5 1.3 bitcast_dynamic-update-slice_fusion.5
  125.8 0.6 fusion.25
  126.4 1.3 bitcast_dynamic-update-slice_fusion.5
  127.7 19.7 %custom-call.5 = f32[2,128,128]{1,2,0:T(8,128)S(1)} custom-call(f32[2,128,128]{2,1,0:T(8,128)S(1)} %get-tuple-element.18), custom_call_target="InvertDiagBlocksLowerTriangular" | custom-call | tf_op jit(solution)/shard_map/triangular_solve/custom-call.1 | solution.py:33
  147.4 1.9 copy.27
  149.3 73.5 %fusion = f32[16,256,2048]{1,2,0:T(8,128)} fusion(f32[16,256,2048]{1,2,0:T(8,128)} %bitcast.82, f32[256,2048]{0,1:T(8,128)S(1)} %copy.27, pred[16]{0:T(512)(128)(4,1)S(1)} %get-tuple-element.53, pred[16]{0:T(512)(128)(4,1)S(1)} %get-tuple-element.54, f32[2,16,1,256,256]{4,3,1,2,0:T(8,128)} %bitcast.86, f32[256,2048]{1,0:T(8,128)} %all-reduce.5.cloned.1.call-done), kind=kOutput, calls=%fused_computation.5 | convolution fusion | flops 25794969600 | bytes 75497504 | tf_op jit(solution)/shard_map/rab,bc->rac/dot_general | solution.py:37
  222.9 1.7 slice_bitcast_fusion.4
  224.6 1.1 fusion.4
  225.7 1.8 convolution_subtract_fusion
  227.5 1.1 fusion.11
  228.6 1.5 maximum_select_fusion.1
  230.1 89.0 %all-reduce.7.cloned.1.call-done = f32[256,2048]{1,0:T(8,128)} async-done(((f32[256,2048]{1,0:T(8,128)}), f32[256,2048]{1,0:T(8,128)}) %all-reduce.7.cloned.1.call-update) | async-done | bytes 2097168 | tf_op jit(solution)/shard_map/psum | solution.py:13
  319.1 58.3 %convolution_bitcast_fusion = f32[16,256,2048]{1,2,0:T(8,128)} fusion(f32[2,16,1,256,256]{4,3,1,2,0:T(8,128)} %bitcast.87, f32[256,2048]{1,0:T(8,128)} %all-reduce.7.cloned.1.call-done), kind=kOutput, calls=%fused_computation.6 | convolution fusion | flops 25769803776 | bytes 39845888 | tf_op jit(solution)/shard_map/rab,bc->rac/dot_general | solution.py:37
  377.4 1.8 copy.33
  379.2 18.5 %fusion.1 = f32[8,256,2048]{1,2,0:T(8,128)} fusion(f32[16,256,2048]{1,2,0:T(8,128)} %convolution_bitcast_fusion, f32[16,256,2048]{1,2,0:T(8,128)} %fusion, f32[256,2048]{0,1:T(8,128)} %copy.33, pred[8]{0:T(512)(128)(4,1)S(1)} %bitcast.93, pred[8]{0:T(512)(128)(4,1)S(1)} %bitcast.92), kind=kLoop, calls=%fused_computation.9 | loop fusion | flops 12582912 | bytes 52428816 | tf_op jit(solution)/shard_map/jit(_where)/select_n | solution.py:42
  397.8 16.4 %copy.34 = f32[8,1,256,1,4,512]{5,2,0,3,1,4:T(8,128)} copy(f32[8,1,256,1,4,512]{2,5,4,0,3,1:T(8,128)} %bitcast.83) | data formatting | bytes 33554432 | tf_op jit(solution)/shard_map/reshape | solution.py:58
  414.1 7.2 all-to-all-start
  421.3 0.0 all-reduce.9.cloned.1.call-start
  421.4 0.1 constant_dynamic-update-slice_fusion.1
  421.6 1.4 copy-done.2
  423.0 0.1 constant_dynamic-update-slice_fusion
  423.1 4.6 broadcast_select_fusion.1
  427.8 5.4 copy.41
  433.2 5.3 copy.42
  438.5 127.6 %all-reduce.9.cloned.1.call-done = (f32[512,8,1,256]{0,3,2,1:T(8,128)}, f32[512,8,1,256]{0,3,2,1:T(8,128)}) async-done(((f32[512,8,1,256]{0,3,2,1:T(8,128)}, f32[512,8,1,256]{0,3,2,1:T(8,128)}), (f32[512,8,1,256]{0,3,2,1:T(8,128)}, f32[512,8,1,256]{0,3,2,1:T(8,128)})) %all-reduce.9.cloned.1.call-update) | async-done | bytes 8388624 | tf_op jit(solution)/shard_map/psum | solution.py:13
  566.2 4.7 pad_maximum_fusion
  570.8 58.3 %convolution_multiply_fusion = f32[4096,2048]{1,0:T(8,128)} fusion(f32[512,4096]{0,1:T(8,128)S(1)} %bitcast.90, f32[512,2048]{1,0:T(8,128)S(1)} %copy-done.4), kind=kOutput, calls=%fused_computation.7 | convolution fusion | flops 51547996160 | bytes 46137344 | tf_op jit(solution)/shard_map/dot_general | solution.py:53
  629.2 48.3 %reshape.85 = f32[16,1,256,8,1,256]{5,4,3,2,1,0:T(1,128)} reshape(f32[4096,2048]{1,0:T(8,128)} %convolution_multiply_fusion) | data formatting | bytes 67108864 | tf_op jit(solution)/shard_map/reshape | solution.py:56
  677.5 106.6 %all-to-all-done = f32[8,1,256,1,4,512]{5,2,0,3,1,4:T(8,128)} async-done(((f32[8,1,256,1,4,512]{5,2,0,3,1,4:T(8,128)}), f32[8,1,256,1,4,512]{5,2,0,3,1,4:T(8,128)}, u32[]{:S(2)}, u32[]{:S(2)}) %all-to-all-start) | async-done | bytes 16777248 | tf_op jit(solution)/shard_map/all_to_all | solution.py:59
  784.1 19.9 %copy.36 = f32[8,4,256,1,1,512]{5,4,3,2,1,0:T(1,128)} copy(f32[8,4,256,1,1,512]{5,2,0,1,4,3:T(8,128)} %bitcast.22) | data formatting | bytes 33554432
  (23 shorter events, 0.2 us)
Async XLA Ops:
  7.2 140.2 %all-reduce.5.cloned.1.call-start = ((), (), s32[]{:S(2)}) async-start(), calls=%async_computation.1 | async-start | bytes 4194304 | tf_op jit(solution)/shard_map/psum | solution.py:13
  44.8 274.3 %all-reduce.7.cloned.1.call-start = ((), (), s32[]{:S(2)}) async-start(), calls=%async_computation.2 | async-start | bytes 4194304 | tf_op jit(solution)/shard_map/psum | solution.py:13
  319.1 58.3 %copy-start.1 = (f32[256,2048]{1,0:T(8,128)S(1)}, f32[256,2048]{1,0:T(8,128)}, u32[]{:S(2)}) copy-start(f32[256,2048]{1,0:T(8,128)} %all-reduce.7.cloned.1.call-done) | copy-start | bytes 6291460
  414.1 7.3 copy-start
  414.1 370.0 %all-to-all-start = ((f32[8,1,256,1,4,512]{5,2,0,3,1,4:T(8,128)}), f32[8,1,256,1,4,512]{5,2,0,3,1,4:T(8,128)}, u32[]{:S(2)}, u32[]{:S(2)}) async-start(f32[8,1,256,1,4,512]{5,2,0,3,1,4:T(8,128)} %copy.34), calls=%async_computation | async-start | bytes 33554432 | tf_op jit(solution)/shard_map/all_to_all | solution.py:59
  421.3 144.8 %all-reduce.9.cloned.1.call-start = ((), (), s32[]{:S(2)}) async-start(), calls=%async_computation.3 | async-start | bytes 16777216 | tf_op jit(solution)/shard_map/psum | solution.py:13
  421.4 1.6 copy-start.2
  423.1 4.7 copy-start.3
  566.2 4.7 copy-start.4
Sparse Core Ops, SparseCore 0:
  44.9 88.8 all-reduce.4
  230.2 88.8 all-reduce.6
  438.6 127.4 all-reduce.8
where the time goes:
time: 823 us; the launch traced here: 811 us
  waiting for transfers between devices  323 us (39%)
  local copies, waits for them, and re-layouts  197 us (24%)
  matrix products  197 us (24%)
  other arithmetic  71.2 us (9%)
  between operations  14.2 us (2%)
    psum x3, waiting for transfers between devices, from_root(): return lax.psum(kept, axis)  217 us
    dot_general x2, matrix products, per_device(): jnp.einsum('rab,bc->rac', column_part, solved, precision=lax.Precision.HI...  132 us
    all_to_all x1, waiting for transfers between devices, per_device(): lax.all_to_all(finished, 'row', split_axis=4, concat_axis=1, tiled=True)  107 us
    unnamed x14, local copies, waits for them, and re-layouts  101 us
    dot_general x1, matrix products, per_device(): lax.dot_general(row_panels, stacked, (((0,), (0,)), ((), ())), precision=...  58.3 us
    reshape x1, local copies, waits for them, and re-layouts, per_device(): (gram * (1.0 / (STEPS * BLK))).reshape(blocks_rows, 1, width, blocks_cols...  48.3 us
    another operation x4, other arithmetic, per_device(): lax.linalg.triangular_solve(diagonal, slab, left_side=True, lower=True)  40.4 us
    select_n x1, other arithmetic, per_device(): jnp.where(below, updated, jnp.where(here, solved[None], matrix_rows))  18.5 us
  transfers between devices with their start and end apart: 4, of which 3 were waited for; matrix products, arithmetic and copies ran while one was open for 28% of the time, Pallas kernels for 0%

commit v1 on v0

--- a/solution.py
+++ b/solution.py
@@ -6,6 +6,12 @@
 BLK = 256
 K = 30
 STEPS = 2
+
+
+def swap_blocks(x, axis, split, join):
+    pieces = jnp.split(x, lax.axis_size(axis), axis=split)
+    got = lax.all_to_all(jnp.stack(pieces), axis, 0, 0)
+    return jnp.concatenate(got, axis=join)
 
 
 def from_root(value, axis, source):
@@ -56,7 +62,7 @@
     gram = (gram * (1.0 / (STEPS * BLK))).reshape(blocks_rows, 1, width, blocks_cols, 1, width)
     finished_count = (K + STEPS) // row_count
     finished = matrix_rows[:finished_count].reshape(finished_count, 1, width, 1, row_count, -1)
-    moved = lax.all_to_all(finished, "row", split_axis=4, concat_axis=1, tiled=True)
+    moved = swap_blocks(finished, "row", 4, 1)
     return (gram, moved)
 
 

time: 823 us -> 880 us (1.069)
  local copies, waits for them, and re-layouts: 197 us -> 239 us
  other arithmetic: 71.2 us -> 85.1 us
    unnamed x14 -> x19, local copies, waits for them, and re-layouts: 101 us -> 153 us
    another operation x0 -> x1, other arithmetic: none -> 20.4 us  [swap_blocks(): got = lax.all_to_all(jnp.stack(pieces), axis, 0, 0)]
    reshape x1 -> x0, local copies, waits for them, and re-layouts: 16.4 us -> none  [per_device(): matrix_rows[:finished_count]]
  transfers between devices with their start and end apart: 4 -> 4, of which waited for: 3 -> 3; matrix products, arithmetic and copies ran while one was open for 28% -> 26% of each run, Pallas kernels for 0% -> 0%
where the time goes in v1:
time: 880 us; the launch traced here: 866 us
  waiting for transfers between devices  323 us (37%)
  local copies, waits for them, and re-layouts  239 us (27%)
  matrix products  197 us (22%)
  other arithmetic  85.1 us (10%)
  between operations  14.3 us (2%)
    psum x3, waiting for transfers between devices, from_root(): return lax.psum(kept, axis)  217 us
    unnamed x19, local copies, waits for them, and re-layouts  153 us
    dot_general x2, matrix products, per_device(): jnp.einsum('rab,bc->rac', column_part, solved, precision=lax.Precision.HI...  132 us
    all_to_all x1, waiting for transfers between devices, swap_blocks(): got = lax.all_to_all(jnp.stack(pieces), axis, 0, 0)  107 us
    dot_general x1, matrix products, per_device(): lax.dot_general(row_panels, stacked, (((0,), (0,)), ((), ())), precision=...  58.3 us
    reshape x1, local copies, waits for them, and re-layouts, per_device(): (gram * (1.0 / (STEPS * BLK))).reshape(blocks_rows, 1, width, blocks_cols...  48.3 us
    another operation x4, other arithmetic, per_device(): lax.linalg.triangular_solve(diagonal, slab, left_side=True, lower=True)  40.4 us
    another operation x1, other arithmetic, swap_blocks(): got = lax.all_to_all(jnp.stack(pieces), axis, 0, 0)  20.4 us
  transfers between devices with their start and end apart: 4, of which 3 were waited for; matrix products, arithmetic and copies ran while one was open for 26% of the time, Pallas kernels for 0%

profile of v1, /device:TPU:0, one launch (start us, length us, event | category | flops | bytes accessed | tf_op | source)
XLA Modules:
  0.0 866.5 jit_solution(17774296273174680836)
XLA Ops:
  7.2 1.1 fusion.9
  8.4 4.0 while.4
  8.4 0.6 fusion.25
  9.0 1.4 bitcast_dynamic-update-slice_fusion.4
  11.0 1.4 bitcast_dynamic-update-slice_fusion.4
  12.4 19.7 %custom-call.4 = f32[2,128,128]{1,2,0:T(8,128)S(1)} custom-call(f32[2,128,128]{2,1,0:T(8,128)S(1)} %get-tuple-element.17), custom_call_target="InvertDiagBlocksLowerTriangular" | custom-call | tf_op jit(solution)/shard_map/triangular_solve/custom-call.1 | solution.py:39
  32.1 7.2 slice_reduce_fusion
  39.2 0.9 copy.58
  40.1 1.1 fusion.6
  41.2 1.0 convolution_subtract_fusion.1
  42.2 1.1 fusion.13
  43.3 1.5 maximum_select_fusion
  44.8 79.1 %copy.30 = f32[16,1,256,8,1,256]{2,5,3,0,4,1:T(8,128)} copy(f32[16,1,256,8,1,256]{5,4,3,2,1,0:T(1,128)} %param.4) | data formatting | bytes 67108864 | tf_op args[0]
  124.0 3.8 while.5
  124.0 0.6 fusion.26
  124.6 1.3 bitcast_dynamic-update-slice_fusion.5
  125.9 0.6 fusion.26
  126.5 1.3 bitcast_dynamic-update-slice_fusion.5
  127.8 19.7 %custom-call.5 = f32[2,128,128]{1,2,0:T(8,128)S(1)} custom-call(f32[2,128,128]{2,1,0:T(8,128)S(1)} %get-tuple-element.18), custom_call_target="InvertDiagBlocksLowerTriangular" | custom-call | tf_op jit(solution)/shard_map/triangular_solve/custom-call.1 | solution.py:39
  147.5 1.9 copy.33
  149.5 73.5 %fusion = f32[16,256,2048]{1,2,0:T(8,128)} fusion(f32[16,256,2048]{1,2,0:T(8,128)} %bitcast.85, f32[256,2048]{0,1:T(8,128)S(1)} %copy.33, pred[16]{0:T(512)(128)(4,1)S(1)} %get-tuple-element.57, pred[16]{0:T(512)(128)(4,1)S(1)} %get-tuple-element.58, f32[2,16,1,256,256]{4,3,1,2,0:T(8,128)} %bitcast.94, f32[256,2048]{1,0:T(8,128)} %all-reduce.5.cloned.1.call-done), kind=kOutput, calls=%fused_computation.5 | convolution fusion | flops 25794969600 | bytes 75497504 | tf_op jit(solution)/shard_map/rab,bc->rac/dot_general | solution.py:43
  223.0 1.7 slice_bitcast_fusion.4
  224.7 1.1 fusion.4
  225.8 1.8 convolution_subtract_fusion
  227.6 1.1 fusion.11
  228.7 1.5 maximum_select_fusion.1
  230.2 89.0 %all-reduce.7.cloned.1.call-done = f32[256,2048]{1,0:T(8,128)} async-done(((f32[256,2048]{1,0:T(8,128)}), f32[256,2048]{1,0:T(8,128)}) %all-reduce.7.cloned.1.call-update) | async-done | bytes 2097168 | tf_op jit(solution)/shard_map/psum | solution.py:19
  319.2 58.3 %convolution_bitcast_fusion = f32[16,256,2048]{1,2,0:T(8,128)} fusion(f32[2,16,1,256,256]{4,3,1,2,0:T(8,128)} %bitcast.95, f32[256,2048]{1,0:T(8,128)} %all-reduce.7.cloned.1.call-done), kind=kOutput, calls=%fused_computation.6 | convolution fusion | flops 25769803776 | bytes 39845888 | tf_op jit(solution)/shard_map/rab,bc->rac/dot_general | solution.py:43
  377.5 1.8 copy.39
  379.3 12.1 %fusion.1 = f32[8,256,2048]{1,2,0:T(8,128)S(1)} fusion(f32[16,256,2048]{1,2,0:T(8,128)} %convolution_bitcast_fusion, f32[16,256,2048]{1,2,0:T(8,128)} %fusion, f32[256,2048]{0,1:T(8,128)} %copy.39, pred[8]{0:T(512)(128)(4,1)S(1)} %bitcast.101, pred[8]{0:T(512)(128)(4,1)S(1)} %bitcast.100), kind=kLoop, calls=%fused_computation.9 | loop fusion | flops 12582912 | bytes 52428816 | tf_op jit(solution)/shard_map/jit(_where)/select_n | solution.py:48
  391.4 6.0 fusion.16
  397.4 10.9 %copy.54 = f32[8,1,256,1,1,512]{5,4,3,2,1,0:T(1,128)} copy(f32[8,1,256,1,1,512]{2,5,4,0,3,1:T(8,128)} %get-tuple-element.47) | data formatting | bytes 8388608
  408.3 10.9 %copy.55 = f32[8,1,256,1,1,512]{5,4,3,2,1,0:T(1,128)} copy(f32[8,1,256,1,1,512]{2,5,4,0,3,1:T(8,128)} %get-tuple-element.49) | data formatting | bytes 8388608
  419.2 10.9 %copy.56 = f32[8,1,256,1,1,512]{5,4,3,2,1,0:T(1,128)} copy(f32[8,1,256,1,1,512]{2,5,4,0,3,1:T(8,128)} %get-tuple-element.48) | data formatting | bytes 8388608
  430.1 10.9 %copy.57 = f32[8,1,256,1,1,512]{5,4,3,2,1,0:T(1,128)} copy(f32[8,1,256,1,1,512]{2,5,4,0,3,1:T(8,128)} %get-tuple-element.50) | data formatting | bytes 8388608
  441.0 20.4 %pad_maximum_fusion = f32[4,8,1,256,1,1,512]{6,5,4,3,2,1,0:T(1,128)} fusion(f32[1,8,1,256,1,1,512]{6,5,4,3,2,1,0:T(1,128)} %bitcast.93, f32[1,8,1,256,1,1,512]{6,5,4,3,2,1,0:T(1,128)} %bitcast.92, f32[1,8,1,256,1,1,512]{6,5,4,3,2,1,0:T(1,128)} %bitcast.91, f32[1,8,1,256,1,1,512]{6,5,4,3,2,1,0:T(1,128)} %bitcast.90), kind=kLoop, calls=%fused_computation.10 | loop fusion | flops 12582912 | bytes 33554432 | tf_op jit(solution)/shard_map/stack | solution.py:13
  461.3 7.2 all-to-all-start
  468.8 1.4 copy-done.2
  470.4 4.6 broadcast_select_fusion.1
  475.0 5.4 copy.50
  480.4 5.3 copy.51
  485.7 127.7 %all-reduce.9.cloned.1.call-done = (f32[512,8,1,256]{0,3,2,1:T(8,128)}, f32[512,8,1,256]{0,3,2,1:T(8,128)}) async-done(((f32[512,8,1,256]{0,3,2,1:T(8,128)}, f32[512,8,1,256]{0,3,2,1:T(8,128)}), (f32[512,8,1,256]{0,3,2,1:T(8,128)}, f32[512,8,1,256]{0,3,2,1:T(8,128)})) %all-reduce.9.cloned.1.call-update) | async-done | bytes 8388624 | tf_op jit(solution)/shard_map/psum | solution.py:19
  613.4 4.7 pad_maximum_fusion.1
  618.1 58.3 %convolution_multiply_fusion = f32[4096,2048]{1,0:T(8,128)} fusion(f32[512,4096]{0,1:T(8,128)S(1)} %bitcast.98, f32[512,2048]{1,0:T(8,128)S(1)} %copy-done.4), kind=kOutput, calls=%fused_computation.7 | convolution fusion | flops 51547996160 | bytes 46137344 | tf_op jit(solution)/shard_map/dot_general | solution.py:59
  676.4 48.3 %reshape.93 = f32[16,1,256,8,1,256]{5,4,3,2,1,0:T(1,128)} reshape(f32[4096,2048]{1,0:T(8,128)} %convolution_multiply_fusion) | data formatting | bytes 67108864 | tf_op jit(solution)/shard_map/reshape | solution.py:62
  724.8 106.6 %all-to-all-done = f32[4,8,1,256,1,1,512]{6,5,4,3,2,1,0:T(1,128)} async-done(((f32[4,8,1,256,1,1,512]{6,5,4,3,2,1,0:T(1,128)}), f32[4,8,1,256,1,1,512]{6,5,4,3,2,1,0:T(1,128)}, u32[]{:S(2)}, u32[]{:S(2)}) %all-to-all-start) | async-done | bytes 16777248 | tf_op jit(solution)/shard_map/all_to_all | solution.py:13
  831.4 8.1 copy.60
  839.4 20.3 %copy.45 = f32[8,4,256,1,1,512]{5,4,3,2,1,0:T(1,128)} copy(f32[8,4,256,1,1,512]{5,2,0,1,4,3:T(8,128)S(1)} %bitcast.87) | data formatting | bytes 33554432
  (29 shorter events, 1.2 us)
Async XLA Ops:
  7.2 140.4 %all-reduce.5.cloned.1.call-start = ((), (), s32[]{:S(2)}) async-start(), calls=%async_computation.1 | async-start | bytes 4194304 | tf_op jit(solution)/shard_map/psum | solution.py:19
  44.8 274.4 %all-reduce.7.cloned.1.call-start = ((), (), s32[]{:S(2)}) async-start(), calls=%async_computation.2 | async-start | bytes 4194304 | tf_op jit(solution)/shard_map/psum | solution.py:19
  319.2 58.3 %copy-start.1 = (f32[256,2048]{1,0:T(8,128)S(1)}, f32[256,2048]{1,0:T(8,128)}, u32[]{:S(2)}) copy-start(f32[256,2048]{1,0:T(8,128)} %all-reduce.7.cloned.1.call-done) | copy-start | bytes 6291460
  461.3 7.3 copy-start
  461.3 370.0 %all-to-all-start = ((f32[4,8,1,256,1,1,512]{6,5,4,3,2,1,0:T(1,128)}), f32[4,8,1,256,1,1,512]{6,5,4,3,2,1,0:T(1,128)}, u32[]{:S(2)}, u32[]{:S(2)}) async-start(f32[4,8,1,256,1,1,512]{6,5,4,3,2,1,0:T(1,128)} %pad_maximum_fusion), calls=%async_computation | async-start | bytes 33554432 | tf_op jit(solution)/shard_map/all_to_all | solution.py:13
  468.6 144.8 %all-reduce.9.cloned.1.call-start = ((), (), s32[]{:S(2)}) async-start(), calls=%async_computation.3 | async-start | bytes 16777216 | tf_op jit(solution)/shard_map/psum | solution.py:19
  468.7 1.6 copy-start.2
  470.4 4.6 copy-start.3
  613.4 4.7 copy-start.4
Sparse Core Ops, SparseCore 0:
  44.9 88.8 all-reduce.4
  230.3 88.8 all-reduce.6
  485.9 127.4 all-reduce.8
